TPU v7x, 32 devices: a whole 2x2x4 slice. The times are simulated.
32 devices in a mesh: dp: 4 (over y, x), sp: 4 (over z), shift: 2 (over core).
Axes of the slice: x: 2, y: 2, z: 4, core: 2. Of those that a mesh axis runs over, the one named last changes fastest.
Arguments:
- query_rows: bfloat16 [8, 1024, 32, 128], P(('shift', 'dp'), 'sp'), parts along dimension 0, may hold values from -6 to 6
- key_rows: bfloat16 [8, 1024, 32, 128], P(('shift', 'dp'), 'sp'), parts along dimension 0, may hold values from -6 to 6
- value_rows: bfloat16 [8, 1024, 32, 128], P(('shift', 'dp'), 'sp'), parts along dimension 0, may hold values from -6 to 6
- out_weight: bfloat16 [8192, 4096], P(('shift', 'dp')), parts along dimension 0, may hold values from -0.09375 to 0.09375
Outputs:
- mixer_out: bfloat16 [8, 1024, 4096], P(('shift', 'dp'), 'sp'), parts along dimension 0
There are 2 independent parts, one for each index of `shift`. A program takes and returns all parts, laid end to end along the dimension named above; each array names one. Nothing has to cross between parts.
All inputs are finite; a program needn't handle non-finite values.
Results may differ from a plain program's by a relative error of at most 0.006.
Values may be sent and summed in bfloat16 or wider, within the bound.
A program may use at most 128 MiB of HBM per device.

v0:
```python
import jax
import jax.numpy as jnp
from jax import lax
from jax.sharding import PartitionSpec as P


def feature_map(values):
    wide = values.astype(jnp.float32)
    return jnp.where(wide > 0.0, wide + 1.0, jnp.exp(jnp.minimum(wide, 0.0))).astype(jnp.bfloat16)


def finish_heads(read, count):
    result = read * count**0.5
    return result.astype(jnp.bfloat16)


def ask_state(features, state, mass):
    top = jnp.einsum(
        "bthd,bhde->bthe", features, state.astype(jnp.bfloat16), preferred_element_type=jnp.float32
    )
    bottom = jnp.einsum(
        "bthd,bhd->bth", features.astype(jnp.float32), mass, precision=lax.Precision.HIGHEST
    )
    return top / (bottom + 0.001)[..., None]


def body(query_rows, key_rows, value_rows, out_weight):
    query_feature, key_feature = (feature_map(query_rows), feature_map(key_rows))
    count = query_rows.shape[1] * lax.axis_size("sp")
    head_query, head_key, head_value = (
        lax.all_to_all(query_feature, "sp", split_axis=2, concat_axis=1, tiled=True),
        lax.all_to_all(key_feature, "sp", split_axis=2, concat_axis=1, tiled=True),
        lax.all_to_all(value_rows, "sp", split_axis=2, concat_axis=1, tiled=True),
    )
    state = (
        jnp.einsum("bthd,bthe->bhde", head_key, head_value, preferred_element_type=jnp.float32)
        / count
    )
    mass = jnp.sum(head_key.astype(jnp.float32), axis=1) / count
    head_read = ask_state(head_query, state, mass)
    read = lax.all_to_all(
        head_read.astype(jnp.bfloat16), "sp", split_axis=1, concat_axis=2, tiled=True
    ).astype(head_read.dtype)
    mixed = finish_heads(read, count)
    mixed = mixed.reshape(mixed.shape[0], mixed.shape[1], -1)
    return jnp.einsum(
        "btw,wv->btv",
        mixed,
        lax.all_gather(out_weight, "dp", axis=0, tiled=True),
        preferred_element_type=jnp.float32,
    ).astype(jnp.bfloat16)


def solution(mesh):
    placed = (
        P(("shift", "dp"), "sp", None, None),
        P(("shift", "dp"), "sp", None, None),
        P(("shift", "dp"), "sp", None, None),
        P(("shift", "dp"), None),
    )
    return jax.shard_map(
        body, mesh=mesh, in_specs=placed, out_specs=P(("shift", "dp"), "sp", None), check_vma=False
    )
```

profile of v0, /device:TPU:0, one launch (start us, length us, event | category | flops | bytes accessed | tf_op | source)
XLA Modules:
  0.0 332.6 jit_solution(15395133279585855644)
XLA Ops:
  8.1 2.6 fusion.5
  10.8 6.3 %all-to-all-start.2 = ((bf16[1,256,32,128]{3,1,0,2:T(8,128)(2,1)}), bf16[1,256,32,128]{3,1,0,2:T(8,128)(2,1)S(1)}, u32[]{:S(2)}, u32[]{:S(2)}) async-start(bf16[1,256,32,128]{3,1,0,2:T(8,128)(2,1)} %fusion.5), calls=%async_computation.2 | async-start | bytes 4194304 | tf_op jit(solution)/shard_map/all_to_all | solution.py:31
  17.1 5.1 %fusion.2 = bf16[1,256,32,128]{3,1,0,2:T(8,128)(2,1)} fusion(bf16[1,256,32,128]{3,2,1,0:T(8,128)(2,1)} %param.5), kind=kLoop, calls=%fused_computation.9 | loop fusion | flops 6291456 | bytes 4194304 | tf_op jit(solution)/shard_map/convert_element_type | solution.py:9
  22.2 43.1 %all-to-all-done.2 = bf16[1,256,32,128]{3,1,0,2:T(8,128)(2,1)S(1)} async-done(((bf16[1,256,32,128]{3,1,0,2:T(8,128)(2,1)}), bf16[1,256,32,128]{3,1,0,2:T(8,128)(2,1)S(1)}, u32[]{:S(2)}, u32[]{:S(2)}) %all-to-all-start.2) | async-done | bytes 2097184 | tf_op jit(solution)/shard_map/all_to_all | solution.py:31
  65.3 1.3 copy-done
  66.6 3.6 %all-to-all-start = ((bf16[1,256,32,128]{3,1,0,2:T(8,128)(2,1)}), bf16[1,256,32,128]{3,1,0,2:T(8,128)(2,1)S(1)}, u32[]{:S(2)}, u32[]{:S(2)}) async-start(bf16[1,256,32,128]{3,1,0,2:T(8,128)(2,1)} %fusion.2), calls=%async_computation | async-start | bytes 4194304 | tf_op jit(solution)/shard_map/all_to_all | solution.py:32
  70.2 3.7 %copy.30 = bf16[1,256,32,128]{3,1,0,2:T(8,128)(2,1)} copy(bf16[1,256,32,128]{3,2,1,0:T(8,128)(2,1)} %param.6) | data formatting | bytes 4194304 | tf_op args[2]
  74.0 44.0 %all-to-all-done = bf16[1,256,32,128]{3,1,0,2:T(8,128)(2,1)S(1)} async-done(((bf16[1,256,32,128]{3,1,0,2:T(8,128)(2,1)}), bf16[1,256,32,128]{3,1,0,2:T(8,128)(2,1)S(1)}, u32[]{:S(2)}, u32[]{:S(2)}) %all-to-all-start) | async-done | bytes 2097184 | tf_op jit(solution)/shard_map/all_to_all | solution.py:32
  118.0 4.6 %all-to-all-start.1 = ((bf16[1,256,32,128]{3,1,0,2:T(8,128)(2,1)}), bf16[1,256,32,128]{3,1,0,2:T(8,128)(2,1)}, u32[]{:S(2)}, u32[]{:S(2)}) async-start(bf16[1,256,32,128]{3,1,0,2:T(8,128)(2,1)} %copy.30), calls=%async_computation.1 | async-start | bytes 4194304 | tf_op jit(solution)/shard_map/all_to_all | solution.py:33
  122.6 3.1 copy.36
  125.8 1.4 copy.68
  127.1 1.8 copy.29
  128.9 41.4 %all-to-all-done.1 = bf16[1,256,32,128]{3,1,0,2:T(8,128)(2,1)} async-done(((bf16[1,256,32,128]{3,1,0,2:T(8,128)(2,1)}), bf16[1,256,32,128]{3,1,0,2:T(8,128)(2,1)}, u32[]{:S(2)}, u32[]{:S(2)}) %all-to-all-start.1) | async-done | bytes 2097184 | tf_op jit(solution)/shard_map/all_to_all | solution.py:33
  170.2 2.9 copy.67
  173.2 1.7 copy.32
  174.9 1.1 convert_reduce_fusion
  176.5 1.7 fusion.28
  178.2 5.4 %fusion.7 = bf16[1,1024,8,128]{1,3,2,0:T(8,128)(2,1)} fusion(bf16[1024,8,128]{2,0,1:T(8,128)(2,1)S(1)} %bitcast.53, f32[1024,8]{0,1:T(8,128)S(1)} %fusion.26, bf16[1024,8,128]{2,1,0:T(8,128)(2,1)} %bitcast.58, bf16[1024,8,128]{2,1,0:T(8,128)(2,1)} %bitcast.57), kind=kOutput, calls=%fused_computation.15 | convolution fusion | flops 539230208 | bytes 8421376 | tf_op jit(solution)/shard_map/bthd,bhde->bthe/dot_general | solution.py:18
  183.6 3.4 %copy.38 = bf16[1,1024,8,128]{3,2,0,1:T(8,128)(2,1)S(1)} copy(bf16[1,1024,8,128]{1,3,2,0:T(8,128)(2,1)} %fusion.7) | data formatting | bytes 4194304 | tf_op jit(solution)/shard_map/convert_element_type | solution.py:42
  187.0 50.2 %all_to_all.54 = bf16[1,1024,8,128]{3,2,0,1:T(8,128)(2,1)S(1)} all-to-all(bf16[1,1024,8,128]{3,2,0,1:T(8,128)(2,1)S(1)} %copy.38), channel_id=1, replica_groups=mesh['dp'=4,'sp'=4,'shift'=2] {'sp'}, dimensions={1} | all-to-all | bytes 4194304 | tf_op jit(solution)/shard_map/all_to_all | solution.py:41
  237.2 1.7 multiply_convert_fusion
  238.9 3.0 copy.40
  241.9 67.1 %all-gather.2.cloned.1.call-done = bf16[4096,4096]{1,0:T(8,128)(2,1)} async-done(((bf16[1024,4096]{1,0:T(8,128)(2,1)}), bf16[4096,4096]{1,0:T(8,128)(2,1)}) %all-gather.2.cloned.1.call-update) | async-done | bytes 33554448 | tf_op jit(solution)/shard_map/all_gather | solution.py:49
  309.0 16.7 %fusion = bf16[1,256,4096]{2,1,0:T(8,128)(2,1)} fusion(bf16[256,4096]{0,1:T(8,128)(2,1)S(1)} %bitcast.50, bf16[4096,4096]{1,0:T(8,128)(2,1)} %all-gather.2.cloned.1.call-done), kind=kOutput, calls=%fused_computation.7 | convolution fusion | flops 8590983168 | bytes 37748736 | tf_op jit(solution)/shard_map/btw,wv->btv/dot_general | solution.py:46
  (11 shorter events, 2.1 us)
Async XLA Ops:
  6.5 1.6 copy-start.3
  6.5 302.5 %all-gather.2.cloned.1.call-start = ((), (), s32[]{:S(2)}) async-start(), calls=%async_computation.4 | async-start | bytes 41943040 | tf_op jit(solution)/shard_map/all_gather | solution.py:49
  10.8 54.5 %all-to-all-start.2 = ((bf16[1,256,32,128]{3,1,0,2:T(8,128)(2,1)}), bf16[1,256,32,128]{3,1,0,2:T(8,128)(2,1)S(1)}, u32[]{:S(2)}, u32[]{:S(2)}) async-start(bf16[1,256,32,128]{3,1,0,2:T(8,128)(2,1)} %fusion.5), calls=%async_computation.2 | async-start | bytes 4194304 | tf_op jit(solution)/shard_map/all_to_all | solution.py:31
  65.3 1.3 copy-start
  66.6 51.3 %all-to-all-start = ((bf16[1,256,32,128]{3,1,0,2:T(8,128)(2,1)}), bf16[1,256,32,128]{3,1,0,2:T(8,128)(2,1)S(1)}, u32[]{:S(2)}, u32[]{:S(2)}) async-start(bf16[1,256,32,128]{3,1,0,2:T(8,128)(2,1)} %fusion.2), calls=%async_computation | async-start | bytes 4194304 | tf_op jit(solution)/shard_map/all_to_all | solution.py:32
  118.0 52.3 %all-to-all-start.1 = ((bf16[1,256,32,128]{3,1,0,2:T(8,128)(2,1)}), bf16[1,256,32,128]{3,1,0,2:T(8,128)(2,1)}, u32[]{:S(2)}, u32[]{:S(2)}) async-start(bf16[1,256,32,128]{3,1,0,2:T(8,128)(2,1)} %copy.30), calls=%async_computation.1 | async-start | bytes 4194304 | tf_op jit(solution)/shard_map/all_to_all | solution.py:33
  174.9 1.6 copy-start.1
  176.0 2.2 copy-start.2
Sparse Core Ops, SparseCore 0:
  9.2 299.7 all-gather.1
where the time goes:
time: 333 us
  waiting for transfers between devices  196 us (59%)
  blocking collectives  50.2 us (15%)
  matrix products  23.8 us (7%)
  local copies, waits for them, and re-layouts  23.6 us (7%)
  starting transfers between devices  14.6 us (4%)
  between operations  13.5 us (4%)
  other arithmetic  10.6 us (3%)
    all_gather x1, waiting for transfers between devices, body(): lax.all_gather(out_weight, 'dp', axis=0, tiled=True)  67.1 us
    all_to_all x1, blocking collectives, body(): lax.all_to_all(head_read.astype(jnp.bfloat16), 'sp', split_axis=1, concat...  50.2 us
    all_to_all x1, waiting for transfers between devices, body(): lax.all_to_all(key_feature, 'sp', split_axis=2, concat_axis=1, tiled=True)  44 us
    all_to_all x1, waiting for transfers between devices, body(): lax.all_to_all(query_feature, 'sp', split_axis=2, concat_axis=1, tiled=True)  43.1 us
    all_to_all x1, waiting for transfers between devices, body(): lax.all_to_all(value_rows, 'sp', split_axis=2, concat_axis=1, tiled=True)  41.4 us
    dot_general x1, matrix products, body(): jnp.einsum('btw,wv->btv', mixed, lax.all_gather(out_weight, 'dp', axis=0,...  16.7 us
    convert_element_type x2, other arithmetic, feature_map(): jnp.where(wide > 0.0, wide + 1.0, jnp.exp(jnp.minimum(wide, 0.0)))  7.71 us
  transfers between devices with their start and end apart: 4, of which 4 were waited for; matrix products, arithmetic and copies ran while one was open for 12% of the time, Pallas kernels for 0%

commit v1 on v0

v1 whole, which is shorter than its diff:
```python
import jax
import jax.numpy as jnp
from jax import lax
from jax.sharding import PartitionSpec as P


def feature_map(values):
    wide = values.astype(jnp.float32)
    return jnp.where(wide > 0.0, wide + 1.0, jnp.exp(jnp.minimum(wide, 0.0))).astype(jnp.bfloat16)


def plain_body(query_rows, key_rows, value_rows, out_weight):
    query_feature, key_feature = (feature_map(query_rows), feature_map(key_rows))
    count = query_rows.shape[1] * lax.axis_size("sp")
    state = (
        jnp.einsum("bthd,bthe->bhde", key_feature, value_rows, preferred_element_type=jnp.float32)
        / count
    )
    mass = jnp.sum(key_feature.astype(jnp.float32), axis=1) / count
    state = lax.psum(state.astype(jnp.bfloat16), "sp")
    mass = lax.psum(mass, "sp")
    top = jnp.einsum("bthd,bhde->bthe", query_feature, state, preferred_element_type=jnp.float32)
    bottom = jnp.einsum(
        "bthd,bhd->bth", query_feature.astype(jnp.float32), mass, precision=lax.Precision.HIGHEST
    )
    mixed = (top / (bottom + 0.001)[..., None] * count**0.5).astype(jnp.bfloat16)
    mixed = mixed.reshape(mixed.shape[0], mixed.shape[1], -1)
    mine = lax.all_to_all(mixed, "dp", split_axis=2, concat_axis=0, tiled=True)
    part = jnp.einsum("btw,wv->btv", mine, out_weight, preferred_element_type=jnp.float32)
    return lax.psum_scatter(part.astype(jnp.bfloat16), "dp", scatter_dimension=0, tiled=True)


def solution(mesh):
    placed = (
        P(("shift", "dp"), "sp", None, None),
        P(("shift", "dp"), "sp", None, None),
        P(("shift", "dp"), "sp", None, None),
        P(("shift", "dp"), None),
    )
    return jax.shard_map(
        plain_body, mesh=mesh, in_specs=placed, out_specs=P(("shift", "dp"), "sp", None), check_vma=False
    )
```

time: 333 us -> 272 us (0.82)
  waiting for transfers between devices: 196 us -> 107 us
  local copies, waits for them, and re-layouts: 23.6 us -> 46.7 us
  other arithmetic: 10.6 us -> 29.8 us
  starting transfers between devices: 14.6 us -> 0.04 us
    all_to_all x3 -> x0, waiting for transfers between devices: 128 us -> none  [the longest x1 44 us: body(): lax.all_to_all(key_feature, 'sp', split_axis=2, concat_axis=1, tiled=True)]
    unnamed x1 -> x3, waiting for transfers between devices: 0.71 us -> 84.3 us
    all_gather x1 -> x0, waiting for transfers between devices: 67.1 us -> none  [body(): lax.all_gather(out_weight, 'dp', axis=0, tiled=True)]
    reshape x0 -> x1, local copies, waits for them, and re-layouts: none -> 25.1 us  [plain_body(): mixed = mixed.reshape(mixed.shape[0], mixed.shape[1], -1)]
    psum x0 -> x1, waiting for transfers between devices: none -> 23.1 us  [plain_body(): state = lax.psum(state.astype(jnp.bfloat16), 'sp')]
    unnamed x0 -> x1, other arithmetic: none -> 22.9 us
    psum x0 -> x1, blocking collectives: none -> 21.4 us  [plain_body(): mass = lax.psum(mass, 'sp')]
    all_to_all x1, blocking collectives: 50.2 us -> 30.2 us  [plain_body(): mine = lax.all_to_all(mixed, 'dp', split_axis=2, concat_axis=0, tiled=True)]
  transfers between devices with their start and end apart: 4 -> 2, of which waited for: 4 -> 2; matrix products, arithmetic and copies ran while one was open for 12% -> 4% of each run, Pallas kernels for 0% -> 0%
where the time goes in v1:
time: 272 us; the launch traced here: 271 us
  waiting for transfers between devices  107 us (39%)
  blocking collectives  51.6 us (19%)
  local copies, waits for them, and re-layouts  46.7 us (17%)
  other arithmetic  29.8 us (11%)
  matrix products  22.4 us (8%)
  between operations  13.4 us (5%)
    unnamed x3, waiting for transfers between devices  84.3 us
    all_to_all x1, blocking collectives, plain_body(): mine = lax.all_to_all(mixed, 'dp', split_axis=2, concat_axis=0, tiled=True)  30.2 us
    reshape x1, local copies, waits for them, and re-layouts, plain_body(): mixed = mixed.reshape(mixed.shape[0], mixed.shape[1], -1)  25.1 us
    psum x1, waiting for transfers between devices, plain_body(): state = lax.psum(state.astype(jnp.bfloat16), 'sp')  23.1 us
    unnamed x1, other arithmetic  22.9 us
    psum x1, blocking collectives, plain_body(): mass = lax.psum(mass, 'sp')  21.4 us
    dot_general x1, matrix products, plain_body(): jnp.einsum('btw,wv->btv', mine, out_weight, preferred_element_type=jnp.fl...  14.7 us
    unnamed x6, local copies, waits for them, and re-layouts  13.4 us
  transfers between devices with their start and end apart: 2, of which 2 were waited for; matrix products, arithmetic and copies ran while one was open for 4% of the time, Pallas kernels for 0%

profile of v1, /device:TPU:0, one launch (start us, length us, event | category | flops | bytes accessed | tf_op | source)
XLA Modules:
  0.0 271.4 jit_solution(5975725253797837042)
XLA Ops:
  6.5 0.0 copy-start
  6.5 0.0 all-reduce.3.cloned.1.call-start
  6.5 3.0 %convert_reduce_fusion = (f32[32,128]{1,0:T(8,128)S(1)}, bf16[256,32,128]{2,1,0:T(8,128)(2,1)S(1)}) fusion(bf16[1,256,32,128]{3,2,1,0:T(8,128)(2,1)} %param.5), kind=kLoop, calls=%fused_computation.18 | loop fusion | flops 8384512 | bytes 4210688 | tf_op jit(solution)/shard_map/reduce_sum | solution.py:19
  9.5 0.0 copy-done
  9.5 2.5 multiply_convert_fusion
  12.1 0.0 all-reduce.3.cloned.1.call-update
  12.1 0.0 reduce-scatter.4.cloned.1.call-start
  12.1 4.0 %fusion.13 = bf16[256,32,128]{2,1,0:T(8,128)(2,1)} fusion(bf16[1,256,32,128]{3,2,1,0:T(8,128)(2,1)} %param.4), kind=kLoop, calls=%fused_computation.19 | loop fusion | flops 6291456 | bytes 4194304 | tf_op jit(solution)/shard_map/reshape.5
  16.1 4.3 %copy.16 = bf16[256,32,128]{0,2,1:T(8,128)(2,1)} copy(bf16[256,32,128]{2,1,0:T(8,128)(2,1)} %fusion.13) | data formatting | bytes 4194304 | tf_op jit(solution)/shard_map/reshape.5
  20.4 21.4 %psum.15 = f32[32,128]{1,0:T(8,128)S(1)} all-reduce(f32[32,128]{1,0:T(8,128)S(1)} %broadcast_multiply_fusion), channel_id=1, replica_groups=mesh['dp'=4,'sp'=4,'shift'=2] {'sp'}, use_global_device_ids=true, to_apply=%region_2.3 | all-reduce | flops 4096 | bytes 32768 | tf_op jit(solution)/shard_map/psum | solution.py:21
  41.8 2.5 fusion.24
  44.3 23.1 %all-reduce.3.cloned.1.call-done = bf16[32,128,128]{2,1,0:T(8,128)(2,1)} async-done(((bf16[32,128,128]{2,1,0:T(8,128)(2,1)}), bf16[32,128,128]{2,1,0:T(8,128)(2,1)}) %all-reduce.3.cloned.1.call-update) | async-done | bytes 1048592 | tf_op jit(solution)/shard_map/psum | solution.py:20
  67.4 2.7 fusion.12
  70.1 25.1 %copy.29 = bf16[1,256,4096]{1,0,2:T(2,128)(2,1)} copy(bf16[1,256,4096]{1,2,0:T(8,128)(2,1)S(1)} %bitcast.51) | data formatting | bytes 4194304 | tf_op jit(solution)/shard_map/reshape | solution.py:27
  95.1 0.5 broadcast.38
  95.6 22.9 %reduce.1 = bf16[4096,256]{1,0:T(8,128)(2,1)} reduce(bf16[4096,1,256]{2,1,0:T(2,128)(2,1)} %bitcast.48, bf16[]{:T(256)} %broadcast.38), dimensions={1}, to_apply=%bitcast.46.reduce_sub_computation | reduce | bytes 4194306
  118.5 4.0 %reshape.52 = bf16[4,2,131072]{2,1,0:T(2,128)(2,1)} reshape(bf16[4096,256]{1,0:T(8,128)(2,1)} %reduce.1) | data formatting | bytes 4194304
  122.5 30.2 %all_to_all.18 = bf16[4,2,131072]{2,1,0:T(2,128)(2,1)} all-to-all(bf16[4,2,131072]{2,1,0:T(2,128)(2,1)} %reshape.52), channel_id=1, replica_groups=mesh['dp'=4,'sp'=4,'shift'=2] {'dp'}, dimensions={0} | all-to-all | bytes 4194304 | tf_op jit(solution)/shard_map/all_to_all | solution.py:28
  152.7 5.0 %reshape.53 = bf16[4096,1,256]{2,1,0:T(2,128)(2,1)} reshape(bf16[4,2,131072]{2,1,0:T(2,128)(2,1)} %all_to_all.18) | data formatting | bytes 4194304
  157.7 3.9 %copy.18 = bf16[1,256,4096]{1,2,0:T(8,128)(2,1)} copy(bf16[1,256,4096]{1,0,2:T(2,128)(2,1)} %bitcast.49) | data formatting | bytes 4194304
  161.6 4.0 %copy.13 = bf16[1,256,4,1024]{3,1,2,0:T(8,128)(2,1)} copy(bf16[1,256,4,1024]{1,3,2,0:T(8,128)(2,1)} %bitcast.50) | data formatting | bytes 4194304 | tf_op jit(solution)/shard_map/all_to_all | solution.py:28
  165.5 14.7 %fusion.2 = bf16[4,256,4096]{2,1,0:T(8,128)(2,1)} fusion(bf16[1024,4096]{1,0:T(8,128)(2,1)} %param.7, bf16[1,256,4,1024]{3,1,2,0:T(8,128)(2,1)} %copy.13), kind=kOutput, calls=%fused_computation.2 | convolution fusion | flops 8594128896 | bytes 18874368 | tf_op jit(solution)/shard_map/btw,wv->btv/dot_general | solution.py:29
  180.2 0.0 reduce-scatter.4.cloned.1.call-update
  180.3 84.3 %reduce-scatter.4.cloned.1.call-done = bf16[1,256,4096]{2,1,0:T(8,128)(2,1)} async-done(((bf16[4,256,4096]{2,1,0:T(8,128)(2,1)}), bf16[1,256,4096]{2,1,0:T(8,128)(2,1)}) %reduce-scatter.4.cloned.1.call-update) | async-done | bytes 2097168
  (2 shorter events, 0.0 us)
Async XLA Ops:
  6.5 3.0 %copy-start = (bf16[1,256,32,128]{3,2,1,0:T(8,128)(2,1)S(1)}, bf16[1,256,32,128]{3,2,1,0:T(8,128)(2,1)}, u32[]{:S(2)}) copy-start(bf16[1,256,32,128]{3,2,1,0:T(8,128)(2,1)} %param.6) | copy-start | bytes 6291460
  6.5 60.8 %all-reduce.3.cloned.1.call-start = ((), (), s32[]{:S(2)}) async-start(), calls=%async_computation.2 | async-start | bytes 2097152 | tf_op jit(solution)/shard_map/psum | solution.py:20
  12.1 252.4 %reduce-scatter.4.cloned.1.call-start = ((), (), s32[]{:S(2)}) async-start(), calls=%async_computation.3 | async-start | bytes 10485760
Sparse Core Ops, SparseCore 0:
  12.2 55.1 all-reduce.2
  180.4 84.0 reduce-scatter.3

commit v2 on v1

--- a/solution.py
+++ b/solution.py
@@ -1,6 +1,10 @@
+import functools
+
 import jax
 import jax.numpy as jnp
 from jax import lax
+from jax.experimental import pallas as pl
+from jax.experimental.pallas import tpu as pltpu
 from jax.sharding import PartitionSpec as P
 
 
@@ -30,6 +34,251 @@
     return lax.psum_scatter(part.astype(jnp.bfloat16), "dp", scatter_dimension=0, tiled=True)
 
 
+MESH = pl.DeviceIdType.MESH
+EXTRA = 16
+NT = (((1,), (1,)), ((), ()))
+
+
+def remote(src, dst, send, recv, **where):
+    return pltpu.make_async_remote_copy(
+        src_ref=src, dst_ref=dst, send_sem=send, recv_sem=recv, device_id=where, device_id_type=MESH
+    )
+
+
+def kernel(
+    ND, NS, A, B, count, q_ref, st_ref, w_hbm, out_ref,
+    w, qall, st1, red, stall, mixed, part, r1e, r1o, s2e, s2o, keep, r2e, r2o,
+    wsem, lsem, qs, qr, ss1, rs1, ss2, rs2, e1s, e1r, o1s, o1r, e2s, e2r, o2s, o2r,
+):
+    d, p = lax.axis_index("dp"), lax.axis_index("sp")
+    i, j = lax.div(d, B), lax.rem(d, B)
+    HD, HS, size = q_ref.shape[1], st_ref.shape[2], q_ref.shape[3]
+    half, C = part.shape[0] // 2, part.shape[-1]
+
+    def at(base, r, n):
+        return lax.rem(base + r + n, n)
+
+    barrier = pltpu.get_barrier_semaphore()
+    for rd in range(ND):
+        for rp in range(NS):
+            if rd or rp:
+                pl.semaphore_signal(
+                    barrier, inc=1, device_id={"dp": at(d, rd, ND), "sp": at(p, rp, NS)}, device_id_type=MESH
+                )
+    pl.semaphore_wait(barrier, ND * NS - 1)
+
+    first = []
+    for r in range(1, NS):
+        pp = at(p, r, NS)
+        copy = remote(st_ref.at[:, pp], st1.at[r - 1], ss1.at[r], rs1.at[r], sp=pp)
+        copy.start()
+        first.append(copy)
+    queries = {}
+    for r in range(1, ND):
+        dd = at(d, r, ND)
+        queries[r] = remote(q_ref.at[dd], qall.at[d], qs.at[r], qr.at[r], dp=dd)
+        queries[r].start()
+    own_query = pltpu.make_async_copy(q_ref.at[d], qall.at[d], lsem.at[0])
+    own_query.start()
+    weights = pltpu.make_async_copy(w_hbm, w, wsem)
+    weights.start()
+
+    for copy in first:
+        copy.wait()
+
+    @pl.loop(0, ND)
+    def _(x):
+        total = st_ref[x, p].astype(jnp.float32)
+        for r in range(1, NS):
+            total += st1[r - 1, x].astype(jnp.float32)
+        red[x] = total.astype(red.dtype)
+
+    second = {}
+    for rp in range(NS - 1, -1, -1):
+        for rd in range(ND):
+            if rd or rp:
+                dd, pp = at(d, rd, ND), at(p, rp, NS)
+                second[rd, rp] = remote(
+                    red.at[dd], stall.at[d, p], ss2.at[rd, rp], rs2.at[rd, rp], dp=dd, sp=pp
+                )
+                second[rd, rp].start()
+    own_state = pltpu.make_async_copy(red.at[d], stall.at[d, p], lsem.at[1])
+    own_state.start()
+
+    for rd in range(ND):
+        s = at(d, -rd, ND)
+        if rd:
+            remote(q_ref.at[d], qall.at[s], qs.at[rd], qr.at[rd], dp=s).wait_recv()
+        else:
+            own_query.wait()
+            own_state.wait()
+        for rp in range(NS):
+            if rd or rp:
+                pp = at(p, -rp, NS)
+                remote(red.at[d], stall.at[s, pp], ss2.at[rd, rp], rs2.at[rd, rp], dp=s, sp=pp).wait_recv()
+
+        @pl.loop(0, NS)
+        def _(pp):
+            for k in range(HS):
+                head = pp * HS + k
+                both = stall[s, pp, k]
+                both = jnp.concatenate([both[:size]] + [both[size:]] * (size // EXTRA), axis=0)
+                read = lax.dot_general(qall[s, head], both, NT, preferred_element_type=jnp.float32)
+                read = read[:, :size] / (read[:, size:] + 0.001) * count**0.5
+                mixed[s, :, pl.ds(pl.multiple_of(head * size, size), size)] = read.astype(mixed.dtype)
+
+    weights.wait()
+
+    def e1(c, r):
+        jj = at(j, r, B)
+        return remote(part.at[2 * c, :, jj], r1e.at[c, r - 1], e1s.at[c, r], e1r.at[c, r], dp=i * B + jj)
+
+    def o1(c, r):
+        ii = at(i, r, A)
+        return remote(part.at[2 * c + 1, ii], r1o.at[c, r - 1], o1s.at[c, r], o1r.at[c, r], dp=ii * B + j)
+
+    def e2(c, r):
+        ii = at(i, r, A)
+        return remote(s2e.at[c, ii], r2e.at[c, r - 1], e2s.at[c, r], e2r.at[c, r], dp=ii * B + j)
+
+    def o2(c, r):
+        jj = at(j, r, B)
+        return remote(s2o.at[c, jj], r2o.at[c, r - 1], o2s.at[c, r], o2r.at[c, r], dp=i * B + jj)
+
+    @pl.loop(0, half)
+    def _(c):
+        for odd in range(2):
+            columns = pl.ds(pl.multiple_of((2 * c + odd) * C, C), C)
+
+            @pl.loop(0, ND)
+            def _(s):
+                block = jnp.dot(mixed[s], w[:, columns], preferred_element_type=jnp.float32)
+                part[2 * c + odd, lax.div(s, B), lax.rem(s, B)] = block.astype(part.dtype)
+
+            for r in range(1, A if odd else B):
+                (o1 if odd else e1)(c, r).start()
+
+    @pl.loop(0, half)
+    def _(c):
+        for r in range(1, B):
+            e1(c, r).wait_recv()
+        for r in range(A):
+            ii = at(i, r, A)
+            total = part[2 * c, ii, j].astype(jnp.float32)
+            for k in range(1, B):
+                total += r1e[c, k - 1, ii].astype(jnp.float32)
+            if r:
+                s2e[c, ii] = total.astype(s2e.dtype)
+                e2(c, r).start()
+            else:
+                keep[2 * c] = total
+        for r in range(1, A):
+            o1(c, r).wait_recv()
+        for r in range(B):
+            jj = at(j, r, B)
+            total = part[2 * c + 1, i, jj].astype(jnp.float32)
+            for k in range(1, A):
+                total += r1o[c, k - 1, jj].astype(jnp.float32)
+            if r:
+                s2o[c, jj] = total.astype(s2o.dtype)
+                o2(c, r).start()
+            else:
+                keep[2 * c + 1] = total
+
+    @pl.loop(0, half)
+    def _(c):
+        for odd, n, copies, slots in ((0, A, e2, r2e), (1, B, o2, r2o)):
+            total = keep[2 * c + odd]
+            for r in range(1, n):
+                copies(c, r).wait_recv()
+                total += slots[c, r - 1].astype(jnp.float32)
+            columns = pl.ds(pl.multiple_of((2 * c + odd) * C, C), C)
+            out_ref[:, columns] = total.astype(out_ref.dtype)
+
+    for r in range(1, ND):
+        queries[r].wait_send()
+    for copy in second.values():
+        copy.wait_send()
+
+    @pl.loop(0, half)
+    def _(c):
+        for r in range(1, B):
+            e1(c, r).wait_send()
+            o2(c, r).wait_send()
+        for r in range(1, A):
+            o1(c, r).wait_send()
+            e2(c, r).wait_send()
+
+
+def split_of(n):
+    for a in range(int(n**0.5), 0, -1):
+        if n % a == 0:
+            return a, n // a
+
+
+def kernel_body(query_rows, key_rows, value_rows, out_weight):
+    ND, NS = lax.axis_size("dp"), lax.axis_size("sp")
+    _, T, H, size = query_rows.shape
+    V, rows = out_weight.shape[1], out_weight.shape[0]
+    A, B = split_of(ND)
+    HD, HS, NC = H // ND, H // ND // NS, 8
+    C, half, count = V // NC, NC // 2, T * NS
+    key_feature = feature_map(key_rows)
+    state = jnp.einsum(
+        "bthd,bthe->bhed", key_feature, value_rows, preferred_element_type=jnp.float32
+    )[0] / count
+    mass = jnp.sum(key_feature.astype(jnp.float32), axis=1)[0] / count
+    mass = jnp.broadcast_to(mass[:, None, :].astype(jnp.bfloat16), (H, EXTRA, size))
+    state = jnp.concatenate([state.astype(jnp.bfloat16), mass], axis=1).reshape(ND, NS, HS, size + EXTRA, size)
+    query = feature_map(query_rows)[0].transpose(1, 0, 2).reshape(ND, HD, T, size)
+    bf, block = jnp.bfloat16, (HS, size + EXTRA, size)
+    dma = pltpu.SemaphoreType.DMA
+    out = pl.pallas_call(
+        functools.partial(kernel, ND, NS, A, B, count),
+        out_shape=jax.ShapeDtypeStruct((T, V), bf),
+        in_specs=[
+            pl.BlockSpec(memory_space=pltpu.VMEM),
+            pl.BlockSpec(memory_space=pltpu.VMEM),
+            pl.BlockSpec(memory_space=pl.ANY),
+        ],
+        out_specs=pl.BlockSpec(memory_space=pltpu.VMEM),
+        scratch_shapes=[
+            pltpu.VMEM((rows, V), bf),
+            pltpu.VMEM((ND, HD, T, size), bf),
+            pltpu.VMEM((NS - 1, ND) + block, bf),
+            pltpu.VMEM((ND,) + block, bf),
+            pltpu.VMEM((ND, NS) + block, bf),
+            pltpu.VMEM((ND, T, HD * size), bf),
+            pltpu.VMEM((NC, A, B, T, C), bf),
+            pltpu.VMEM((half, B - 1, A, T, C), bf),
+            pltpu.VMEM((half, A - 1, B, T, C), bf),
+            pltpu.VMEM((half, A, T, C), bf),
+            pltpu.VMEM((half, B, T, C), bf),
+            pltpu.VMEM((NC, T, C), jnp.float32),
+            pltpu.VMEM((half, A - 1, T, C), bf),
+            pltpu.VMEM((half, B - 1, T, C), bf),
+            dma, dma((2,)), dma((ND,)), dma((ND,)), dma((NS,)), dma((NS,)), dma((ND, NS)), dma((ND, NS)),
+            dma((half, B)), dma((half, B)), dma((half, A)), dma((half, A)),
+            dma((half, A)), dma((half, A)), dma((half, B)), dma((half, B)),
+        ],
+        compiler_params=pltpu.CompilerParams(
+            collective_id=0, has_side_effects=True, vmem_limit_bytes=63 * 2**20
+        ),
+    )(query, state, out_weight)
+    return out[None]
+
+
+def body(query_rows, key_rows, value_rows, out_weight):
+    ND, NS = lax.axis_size("dp"), lax.axis_size("sp")
+    batch, T, H, size = query_rows.shape
+    rows, V = out_weight.shape
+    need = 2 * rows * V + 2 * ND * T * V * 2 + 2 * T * V * 8 + 4 * H * T * size * 2
+    fits = batch == 1 and H % (ND * NS) == 0 and V % 1024 == 0 and min(split_of(ND)) > 1
+    fits = fits and size == 128 and T % 16 == 0 and need < 56 * 2**20
+    run = kernel_body if fits else plain_body
+    return run(query_rows, key_rows, value_rows, out_weight)
+
+
 def solution(mesh):
     placed = (
         P(("shift", "dp"), "sp", None, None),
@@ -38,5 +287,5 @@
         P(("shift", "dp"), None),
     )
     return jax.shard_map(
-        plain_body, mesh=mesh, in_specs=placed, out_specs=P(("shift", "dp"), "sp", None), check_vma=False
-    )
+        body, mesh=mesh, in_specs=placed, out_specs=P(("shift", "dp"), "sp", None), check_vma=False
+    )

time: 272 us -> 156 us (0.57)
  Pallas kernels: 0 us -> 143 us
  waiting for transfers between devices: 107 us -> 0 us
  blocking collectives: 51.6 us -> 0 us
  local copies, waits for them, and re-layouts: 46.7 us -> 5.66 us
  other arithmetic: 29.8 us -> 5.03 us
  matrix products: 22.4 us -> 1.56 us
  between operations: 13.4 us -> 0.05 us
    pallas_call x0 -> x1, Pallas kernels: none -> 143 us  [kernel_body(): pl.pallas_call(functools.partial(kernel, ND, NS, A, B, count), out_shape=...]
    unnamed x3 -> x0, waiting for transfers between devices: 84.3 us -> none
    all_to_all x1 -> x0, blocking collectives: 30.2 us -> none  [plain_body(): mine = lax.all_to_all(mixed, 'dp', split_axis=2, concat_axis=0, tiled=True)]
    reshape x1 -> x0, local copies, waits for them, and re-layouts: 25.1 us -> none  [plain_body(): mixed = mixed.reshape(mixed.shape[0], mixed.shape[1], -1)]
    psum x1 -> x0, waiting for transfers between devices: 23.1 us -> none  [plain_body(): state = lax.psum(state.astype(jnp.bfloat16), 'sp')]
    unnamed x1 -> x0, other arithmetic: 22.9 us -> none
    psum x1 -> x0, blocking collectives: 21.4 us -> none  [plain_body(): mass = lax.psum(mass, 'sp')]
    dot_general x4 -> x1, matrix products: 22.4 us -> 1.56 us  [kernel_body(): jnp.einsum('bthd,bthe->bhed', key_feature, value_rows, preferred_element_...]
  transfers between devices with their start and end apart: 2 -> 0, of which waited for: 2 -> 0; matrix products, arithmetic and copies ran while one was open for 4% -> 0% of each run, Pallas kernels for 0% -> 0%
where the time goes in v2:
time: 156 us; the launch traced here: 155 us
  Pallas kernels  143 us (92%)
  local copies, waits for them, and re-layouts  5.66 us (4%)
  other arithmetic  5.03 us (3%)
  matrix products  1.56 us (1%)
    pallas_call x1, Pallas kernels, kernel_body(): pl.pallas_call(functools.partial(kernel, ND, NS, A, B, count), out_shape=...  143 us
    unnamed x5, local copies, waits for them, and re-layouts  3.5 us

profile of v2, /device:TPU:0, one launch (start us, length us, event | category | flops | bytes accessed | tf_op | source)
XLA Modules:
  0.0 155.4 jit_solution(14943124101760395610)
XLA Ops:
  0.0 2.7 %fusion.6 = bf16[32,256,128]{2,0,1:T(8,128)(2,1)S(1)} fusion(bf16[1,256,32,128]{3,2,1,0:T(8,128)(2,1)} %param.4), kind=kLoop, calls=%fused_computation.13 | loop fusion | flops 6291456 | bytes 4194304 | tf_op jit(solution)/shard_map/transpose | solution.py:233
  2.7 0.0 copy-start
  2.7 2.1 %copy.5 = bf16[32,256,128]{2,1,0:T(8,128)(2,1)} copy(bf16[32,256,128]{2,0,1:T(8,128)(2,1)S(1)} %fusion.6) | data formatting | bytes 4194304 | tf_op jit(solution)/shard_map/transpose | solution.py:233
  4.8 0.0 copy-done
  4.8 0.0 copy-start.1
  4.8 1.2 fusion.14
  6.0 0.4 copy-done.1
  6.4 1.6 %multiply_convert_fusion = bf16[32,128,128]{1,2,0:T(8,128)(2,1)S(1)} fusion(bf16[256,32,128]{2,1,0:T(8,128)(2,1)S(1)} %get-tuple-element.5, bf16[256,32,128]{2,1,0:T(8,128)(2,1)S(1)} %bitcast.17), kind=kOutput, calls=%fused_computation.17 | convolution fusion | flops 269484032 | bytes 5242880 | tf_op jit(solution)/shard_map/bthd,bthe->bhed/dot_general | solution.py:227
  8.0 1.1 pad_maximum_fusion.st_ref
  9.2 143.1 %shard_map.46 = bf16[256,4096]{1,0:T(8,128)(2,1)} custom-call(bf16[4,8,256,128]{3,2,1,0:T(8,128)(2,1)} %bitcast.13, bf16[4,4,2,144,128]{4,3,2,1,0:T(8,128)(2,1)} %pad_maximum_fusion.st_ref, bf16[1024,4096]{1,0:T(8,128)(2,1)} %w_hbm.1), custom_call_target="tpu_custom_call" | custom-call | tf_op jit(solution)/shard_map/pallas_call | solution.py:236
  152.2 3.1 %copy.17 = bf16[1,256,4096]{2,1,0:T(8,128)(2,1)} copy(bf16[1,256,4096]{2,1,0:T(8,128)(2,1)} %bitcast.14) | data formatting | bytes 4194304
  (2 shorter events, 0.0 us)
Async XLA Ops:
  2.7 2.1 %copy-start = (bf16[1,256,32,128]{3,2,1,0:T(8,128)(2,1)S(1)}, bf16[1,256,32,128]{3,2,1,0:T(8,128)(2,1)}, u32[]{:S(2)}) copy-start(bf16[1,256,32,128]{3,2,1,0:T(8,128)(2,1)} %param.5) | copy-start | bytes 6291460
  4.8 1.6 %copy-start.1 = (bf16[1,256,32,128]{3,2,1,0:T(8,128)(2,1)S(1)}, bf16[1,256,32,128]{3,2,1,0:T(8,128)(2,1)}, u32[]{:S(2)}) copy-start(bf16[1,256,32,128]{3,2,1,0:T(8,128)(2,1)} %param.6) | copy-start | bytes 6291460

commit v3 on v2

--- a/solution.py
+++ b/solution.py
@@ -46,9 +46,9 @@
 
 
 def kernel(
-    ND, NS, A, B, count, q_ref, st_ref, w_hbm, out_ref,
-    w, qall, st1, red, stall, mixed, part, r1e, r1o, s2e, s2o, keep, r2e, r2o,
-    wsem, lsem, qs, qr, ss1, rs1, ss2, rs2, e1s, e1r, o1s, o1r, e2s, e2r, o2s, o2r,
+    ND, NS, A, B, count, q_hbm, st_ref, w_hbm, out_ref,
+    qraw, qwide, q_ref, w, qall, st1, red, stall, mixed, part, r1e, r1o, s2e, s2o, keep, r2e, r2o,
+    wsem, qsem, lsem, qs, qr, ss1, rs1, ss2, rs2, e1s, e1r, o1s, o1r, e2s, e2r, o2s, o2r,
 ):
     d, p = lax.axis_index("dp"), lax.axis_index("sp")
     i, j = lax.div(d, B), lax.rem(d, B)
@@ -57,6 +57,19 @@
 
     def at(base, r, n):
         return lax.rem(base + r + n, n)
+
+    def twin(r):
+        other, bit = p, 1
+        while bit <= r:
+            if r & bit:
+                other = other + bit - 2 * bit * lax.rem(lax.div(p, bit), 2)
+            bit *= 2
+        return other
+
+    load = pltpu.make_async_copy(q_hbm, qraw, qsem)
+    load.start()
+    weights = pltpu.make_async_copy(w_hbm, w, wsem)
+    weights.start()
 
     barrier = pltpu.get_barrier_semaphore()
     for rd in range(ND):
@@ -67,12 +80,31 @@
                 )
     pl.semaphore_wait(barrier, ND * NS - 1)
 
-    first = []
-    for r in range(1, NS):
-        pp = at(p, r, NS)
-        copy = remote(st_ref.at[:, pp], st1.at[r - 1], ss1.at[r], rs1.at[r], sp=pp)
-        copy.start()
-        first.append(copy)
+    order = list(range(NS - 1, 0, -1))
+    first = {}
+    for rd in range(ND):
+        dd = at(d, rd, ND)
+        for r in order:
+            pp = twin(r)
+            first[rd, r] = remote(
+                st_ref.at[dd, pp], st1.at[r - 1, dd], ss1.at[rd, r], rs1.at[rd, r], sp=pp
+            )
+            first[rd, r].start()
+
+    load.wait()
+    tokens, heads, step = q_ref.shape[2], ND * HD, 1024
+
+    @pl.loop(0, tokens * heads // step)
+    def _(x):
+        rows = pl.ds(pl.multiple_of(x * step, step), step)
+        wide = qraw[rows].astype(jnp.float32)
+        qwide[rows] = jnp.where(wide > 0.0, wide + 1.0, jnp.exp(jnp.minimum(wide, 0.0)))
+
+    @pl.loop(0, ND)
+    def _(x):
+        for k in range(HD):
+            q_ref[x, k] = qwide[pl.ds(x * HD + k, tokens, stride=heads), :].astype(q_ref.dtype)
+
     queries = {}
     for r in range(1, ND):
         dd = at(d, r, ND)
@@ -80,45 +112,39 @@
         queries[r].start()
     own_query = pltpu.make_async_copy(q_ref.at[d], qall.at[d], lsem.at[0])
     own_query.start()
-    weights = pltpu.make_async_copy(w_hbm, w, wsem)
-    weights.start()
-
-    for copy in first:
-        copy.wait()
-
-    @pl.loop(0, ND)
-    def _(x):
-        total = st_ref[x, p].astype(jnp.float32)
-        for r in range(1, NS):
-            total += st1[r - 1, x].astype(jnp.float32)
-        red[x] = total.astype(red.dtype)
 
     second = {}
-    for rp in range(NS - 1, -1, -1):
-        for rd in range(ND):
+    for rd in range(ND):
+        dd = at(d, rd, ND)
+        total = st_ref[dd, p].astype(jnp.float32)
+        for r in order:
+            first[rd, r].wait_recv()
+            total += st1[r - 1, dd].astype(jnp.float32)
+        red[dd] = total.astype(red.dtype)
+        for rp in [0] + order:
             if rd or rp:
-                dd, pp = at(d, rd, ND), at(p, rp, NS)
                 second[rd, rp] = remote(
-                    red.at[dd], stall.at[d, p], ss2.at[rd, rp], rs2.at[rd, rp], dp=dd, sp=pp
+                    red.at[dd], stall.at[d, p], ss2.at[rd, rp], rs2.at[rd, rp], dp=dd, sp=twin(rp)
                 )
                 second[rd, rp].start()
-    own_state = pltpu.make_async_copy(red.at[d], stall.at[d, p], lsem.at[1])
-    own_state.start()
-
-    for rd in range(ND):
-        s = at(d, -rd, ND)
-        if rd:
-            remote(q_ref.at[d], qall.at[s], qs.at[rd], qr.at[rd], dp=s).wait_recv()
-        else:
-            own_query.wait()
-            own_state.wait()
-        for rp in range(NS):
+            else:
+                own_state = pltpu.make_async_copy(red.at[d], stall.at[d, p], lsem.at[1])
+                own_state.start()
+
+    for rp in [0] + order:
+        pp = twin(rp)
+        for rd in range(ND):
+            s = at(d, -rd, ND)
+            if rp == 0 and rd:
+                remote(q_ref.at[d], qall.at[s], qs.at[rd], qr.at[rd], dp=s).wait_recv()
             if rd or rp:
-                pp = at(p, -rp, NS)
                 remote(red.at[d], stall.at[s, pp], ss2.at[rd, rp], rs2.at[rd, rp], dp=s, sp=pp).wait_recv()
-
-        @pl.loop(0, NS)
-        def _(pp):
+            else:
+                own_query.wait()
+                own_state.wait()
+
+        @pl.loop(0, ND)
+        def _(s):
             for k in range(HS):
                 head = pp * HS + k
                 both = stall[s, pp, k]
@@ -197,7 +223,7 @@
 
     for r in range(1, ND):
         queries[r].wait_send()
-    for copy in second.values():
+    for copy in list(first.values()) + list(second.values()):
         copy.wait_send()
 
     @pl.loop(0, half)
@@ -230,19 +256,22 @@
     mass = jnp.sum(key_feature.astype(jnp.float32), axis=1)[0] / count
     mass = jnp.broadcast_to(mass[:, None, :].astype(jnp.bfloat16), (H, EXTRA, size))
     state = jnp.concatenate([state.astype(jnp.bfloat16), mass], axis=1).reshape(ND, NS, HS, size + EXTRA, size)
-    query = feature_map(query_rows)[0].transpose(1, 0, 2).reshape(ND, HD, T, size)
+    query = query_rows.reshape(T * H, size)
     bf, block = jnp.bfloat16, (HS, size + EXTRA, size)
     dma = pltpu.SemaphoreType.DMA
     out = pl.pallas_call(
         functools.partial(kernel, ND, NS, A, B, count),
         out_shape=jax.ShapeDtypeStruct((T, V), bf),
         in_specs=[
-            pl.BlockSpec(memory_space=pltpu.VMEM),
+            pl.BlockSpec(memory_space=pl.ANY),
             pl.BlockSpec(memory_space=pltpu.VMEM),
             pl.BlockSpec(memory_space=pl.ANY),
         ],
         out_specs=pl.BlockSpec(memory_space=pltpu.VMEM),
         scratch_shapes=[
+            pltpu.VMEM((T * H, size), bf),
+            pltpu.VMEM((T * H, size), jnp.float32),
+            pltpu.VMEM((ND, HD, T, size), bf),
             pltpu.VMEM((rows, V), bf),
             pltpu.VMEM((ND, HD, T, size), bf),
             pltpu.VMEM((NS - 1, ND) + block, bf),
@@ -257,7 +286,7 @@
             pltpu.VMEM((NC, T, C), jnp.float32),
             pltpu.VMEM((half, A - 1, T, C), bf),
             pltpu.VMEM((half, B - 1, T, C), bf),
-            dma, dma((2,)), dma((ND,)), dma((ND,)), dma((NS,)), dma((NS,)), dma((ND, NS)), dma((ND, NS)),
+            dma, dma, dma((2,)), dma((ND,)), dma((ND,)), dma((ND, NS)), dma((ND, NS)), dma((ND, NS)), dma((ND, NS)),
             dma((half, B)), dma((half, B)), dma((half, A)), dma((half, A)),
             dma((half, A)), dma((half, A)), dma((half, B)), dma((half, B)),
         ],
@@ -272,9 +301,9 @@
     ND, NS = lax.axis_size("dp"), lax.axis_size("sp")
     batch, T, H, size = query_rows.shape
     rows, V = out_weight.shape
-    need = 2 * rows * V + 2 * ND * T * V * 2 + 2 * T * V * 8 + 4 * H * T * size * 2
+    need = 2 * rows * V + 2 * ND * T * V * 2 + 2 * T * V * 8 + 6 * H * T * size * 2
     fits = batch == 1 and H % (ND * NS) == 0 and V % 1024 == 0 and min(split_of(ND)) > 1
-    fits = fits and size == 128 and T % 16 == 0 and need < 56 * 2**20
+    fits = fits and size == 128 and T % 16 == 0 and T * H % 1024 == 0 and NS & (NS - 1) == 0 and need < 56 * 2**20
     run = kernel_body if fits else plain_body
     return run(query_rows, key_rows, value_rows, out_weight)
 

time: 156 us -> 146 us (0.936)
  Pallas kernels: 143 us -> 137 us
  local copies, waits for them, and re-layouts: 5.66 us -> 3.15 us
    pallas_call x1, Pallas kernels: 143 us -> 137 us  [kernel_body(): pl.pallas_call(functools.partial(kernel, ND, NS, A, B, count), out_shape=...]
    transpose x1 -> x0, other arithmetic: 2.68 us -> none  [kernel_body(): feature_map(query_rows)[0].transpose(1, 0, 2).reshape(ND, HD, T, size)]
    transpose x1 -> x0, local copies, waits for them, and re-layouts: 2.13 us -> none  [kernel_body(): feature_map(query_rows)[0].transpose(1, 0, 2).reshape(ND, HD, T, size)]
    another operation x1, other arithmetic: 1.22 us -> 2.96 us
    unnamed x5 -> x3, local copies, waits for them, and re-layouts: 3.5 us -> 3.13 us
where the time goes in v3:
time: 146 us
  Pallas kernels  137 us (94%)
  other arithmetic  4.07 us (3%)
  local copies, waits for them, and re-layouts  3.15 us (2%)
  matrix products  1.57 us (1%)
    pallas_call x1, Pallas kernels, kernel_body(): pl.pallas_call(functools.partial(kernel, ND, NS, A, B, count), out_shape=...  137 us
    unnamed x3, local copies, waits for them, and re-layouts  3.13 us
    another operation x1, other arithmetic  2.96 us

profile of v3, /device:TPU:0, one launch (start us, length us, event | category | flops | bytes accessed | tf_op | source)
XLA Modules:
  0.0 146.2 jit_solution(9155923042107673293)
XLA Ops:
  0.0 0.0 copy-start
  0.0 3.0 %fusion.10 = (bf16[256,32,128]{2,1,0:T(8,128)(2,1)S(1)}, f32[32,128]{1,0:T(8,128)S(1)}) fusion(bf16[1,256,32,128]{3,2,1,0:T(8,128)(2,1)} %param.5), kind=kLoop, calls=%fused_computation.12 | loop fusion | flops 8384512 | bytes 4210688 | tf_op jit(solution)/shard_map/reshape.1
  3.0 0.0 copy-done
  3.0 1.6 %multiply_convert_fusion = bf16[32,128,128]{1,2,0:T(8,128)(2,1)S(1)} fusion(bf16[256,32,128]{2,1,0:T(8,128)(2,1)S(1)} %get-tuple-element.5, bf16[256,32,128]{2,1,0:T(8,128)(2,1)S(1)} %bitcast.13), kind=kOutput, calls=%fused_computation.10 | convolution fusion | flops 269484032 | bytes 5242880 | tf_op jit(solution)/shard_map/bthd,bthe->bhed/dot_general | solution.py:253
  4.6 1.1 pad_maximum_fusion.st_ref
  5.7 137.4 %shard_map.46 = bf16[256,4096]{1,0:T(8,128)(2,1)} custom-call(bf16[8192,128]{1,0:T(8,128)(2,1)} %bitcast.10, bf16[4,4,2,144,128]{4,3,2,1,0:T(8,128)(2,1)} %pad_maximum_fusion.st_ref, bf16[1024,4096]{1,0:T(8,128)(2,1)} %w_hbm.1), custom_call_target="tpu_custom_call" | custom-call | tf_op jit(solution)/shard_map/pallas_call | solution.py:262
  143.1 3.1 %copy.16 = bf16[1,256,4096]{2,1,0:T(8,128)(2,1)} copy(bf16[1,256,4096]{2,1,0:T(8,128)(2,1)} %bitcast.9) | data formatting | bytes 4194304
  (2 shorter events, 0.0 us)
Async XLA Ops:
  0.0 3.0 %copy-start = (bf16[1,256,32,128]{3,2,1,0:T(8,128)(2,1)S(1)}, bf16[1,256,32,128]{3,2,1,0:T(8,128)(2,1)}, u32[]{:S(2)}) copy-start(bf16[1,256,32,128]{3,2,1,0:T(8,128)(2,1)} %param.6) | copy-start | bytes 6291460

commit v4 on v3

--- a/solution.py
+++ b/solution.py
@@ -247,7 +247,7 @@
     _, T, H, size = query_rows.shape
     V, rows = out_weight.shape[1], out_weight.shape[0]
     A, B = split_of(ND)
-    HD, HS, NC = H // ND, H // ND // NS, 8
+    HD, HS, NC = H // ND, H // ND // NS, 16
     C, half, count = V // NC, NC // 2, T * NS
     key_feature = feature_map(key_rows)
     state = jnp.einsum(
@@ -302,7 +302,7 @@
     batch, T, H, size = query_rows.shape
     rows, V = out_weight.shape
     need = 2 * rows * V + 2 * ND * T * V * 2 + 2 * T * V * 8 + 6 * H * T * size * 2
-    fits = batch == 1 and H % (ND * NS) == 0 and V % 1024 == 0 and min(split_of(ND)) > 1
+    fits = batch == 1 and H % (ND * NS) == 0 and V % 2048 == 0 and min(split_of(ND)) > 1
     fits = fits and size == 128 and T % 16 == 0 and T * H % 1024 == 0 and NS & (NS - 1) == 0 and need < 56 * 2**20
     run = kernel_body if fits else plain_body
     return run(query_rows, key_rows, value_rows, out_weight)

time: 146 us -> 146 us (level)
  no operation moved by 1% of the time
where the time goes in v4:
time: 146 us
  Pallas kernels  137 us (94%)
  other arithmetic  4.07 us (3%)
  local copies, waits for them, and re-layouts  3.15 us (2%)
  matrix products  1.57 us (1%)
    pallas_call x1, Pallas kernels, kernel_body(): pl.pallas_call(functools.partial(kernel, ND, NS, A, B, count), out_shape=...  137 us
    unnamed x3, local copies, waits for them, and re-layouts  3.13 us
    another operation x1, other arithmetic  2.96 us

profile of v4, /device:TPU:0, one launch (start us, length us, event | category | flops | bytes accessed | tf_op | source)
XLA Modules:
  0.0 145.8 jit_solution(9967343616057212787)
XLA Ops:
  0.0 0.0 copy-start
  0.0 3.0 %fusion.10 = (bf16[256,32,128]{2,1,0:T(8,128)(2,1)S(1)}, f32[32,128]{1,0:T(8,128)S(1)}) fusion(bf16[1,256,32,128]{3,2,1,0:T(8,128)(2,1)} %param.5), kind=kLoop, calls=%fused_computation.12 | loop fusion | flops 8384512 | bytes 4210688 | tf_op jit(solution)/shard_map/reshape.1
  3.0 0.0 copy-done
  3.0 1.6 %multiply_convert_fusion = bf16[32,128,128]{1,2,0:T(8,128)(2,1)S(1)} fusion(bf16[256,32,128]{2,1,0:T(8,128)(2,1)S(1)} %get-tuple-element.5, bf16[256,32,128]{2,1,0:T(8,128)(2,1)S(1)} %bitcast.13), kind=kOutput, calls=%fused_computation.10 | convolution fusion | flops 269484032 | bytes 5242880 | tf_op jit(solution)/shard_map/bthd,bthe->bhed/dot_general | solution.py:253
  4.6 1.1 pad_maximum_fusion.st_ref
  5.7 136.9 %shard_map.46 = bf16[256,4096]{1,0:T(8,128)(2,1)} custom-call(bf16[8192,128]{1,0:T(8,128)(2,1)} %bitcast.10, bf16[4,4,2,144,128]{4,3,2,1,0:T(8,128)(2,1)} %pad_maximum_fusion.st_ref, bf16[1024,4096]{1,0:T(8,128)(2,1)} %w_hbm.1), custom_call_target="tpu_custom_call" | custom-call | tf_op jit(solution)/shard_map/pallas_call | solution.py:262
  142.6 3.1 %copy.16 = bf16[1,256,4096]{2,1,0:T(8,128)(2,1)} copy(bf16[1,256,4096]{2,1,0:T(8,128)(2,1)} %bitcast.9) | data formatting | bytes 4194304
  (2 shorter events, 0.0 us)
Async XLA Ops:
  0.0 3.0 %copy-start = (bf16[1,256,32,128]{3,2,1,0:T(8,128)(2,1)S(1)}, bf16[1,256,32,128]{3,2,1,0:T(8,128)(2,1)}, u32[]{:S(2)}) copy-start(bf16[1,256,32,128]{3,2,1,0:T(8,128)(2,1)} %param.6) | copy-start | bytes 6291460
